TPU v7x, 32 devices: a whole 2x2x4 slice. The times are simulated.
32 devices in a mesh: dp: 16 (over z, x, core), tensor: 2 (over y).
Axes of the slice: x: 2, y: 2, z: 4, core: 2. Of those that a mesh axis runs over, the one named last changes fastest.
Arguments:
- query_rows: bfloat16 [6144, 5120], P('dp', 'tensor'), may hold values from -128 to 128
- key_rows: bfloat16 [6144, 5120], P('dp', 'tensor'), may hold values from -5 to 5
- value_rows: bfloat16 [6144, 5120], P('dp', 'tensor'), may hold values from -12 to 12
- action_mask: int32 [16, 384], P('dp'), may hold values from 0 to 1, as said below
- residual: bfloat16 [6144, 5120], P('dp', 'tensor'), may hold values from -100 to 100
- out_weight: bfloat16 [5120, 5120], P(None, 'tensor'), may hold values from -0.078125 to 0.078125
- norm_gain: float32 [5120], P('tensor'), may hold values from 0.1 to 1.9
- upstream: bfloat16 [6144, 5120], P('dp', 'tensor'), may hold values from -6 to 6
- residual_grad: bfloat16 [6144, 5120], P('dp', 'tensor'), may hold values from -2 to 2
Outputs:
- layer_out: bfloat16 [6144, 5120], P('dp', 'tensor')
- grad_residual: bfloat16 [6144, 5120], P('dp', 'tensor')
- grad_query: bfloat16 [6144, 5120], P('dp', 'tensor')
- grad_key: bfloat16 [6144, 5120], P('dp', 'tensor')
- grad_value: bfloat16 [6144, 5120], P('dp', 'tensor')
- grad_out_weight: float32 [5120, 5120], P('dp', 'tensor')
- grad_gain: float32 [5120], P('tensor')
Inputs may be any that keep to these rules, and one draw needn't show every extreme that they name: `action_mask`: each row is a run of zeros followed by a run of ones; the ones number 1 to 192.
All inputs are finite; a program needn't handle non-finite values.
Results may differ from a plain program's by a relative error of at most 0.015.
Values may be sent and summed in bfloat16 or wider, within the bound.
A program may use at most 192 MiB of HBM per device.

v0:
```python
import jax
import jax.numpy as jnp
from jax import lax
from jax.sharding import PartitionSpec as P

D = 5120
HEAD_DIM = 128
LEN = 384
epsilon = 1e-05


def visible(mask_row):
    position = jnp.arange(mask_row.shape[0])
    causal = position[None, :] <= position[:, None]
    observe = mask_row == 0
    return causal | observe[:, None] & observe[None, :]


def shards(
    query_rows,
    key_rows,
    value_rows,
    action_mask,
    residual,
    out_weight,
    norm_gain,
    upstream,
    residual_grad,
):
    seq_count = action_mask.shape[0]
    tok_rows = query_rows.shape[0]
    local_width = query_rows.shape[1]
    head_shape = (seq_count, LEN, local_width // HEAD_DIM, HEAD_DIM)
    query_heads = query_rows.reshape(head_shape)
    key_heads = key_rows.reshape(head_shape)
    value_heads = value_rows.reshape(head_shape)
    score_scale = HEAD_DIM ** (-0.5)
    allowed = jax.vmap(visible)(action_mask)
    scores = (
        jnp.einsum("sqhd,skhd->shqk", query_heads, key_heads, preferred_element_type=jnp.float32)
        * score_scale
    )
    masked = jnp.where(allowed[:, None], scores, -jnp.inf)
    row_top = jnp.max(masked, axis=-1, keepdims=True)
    weights = jnp.exp(masked - row_top)
    chances = weights / jnp.sum(weights, axis=-1, keepdims=True)
    chances_low = chances.astype(jnp.bfloat16)
    attended = jnp.einsum(
        "shqk,skhd->sqhd", chances_low, value_heads, preferred_element_type=jnp.float32
    )
    attended = attended.astype(jnp.bfloat16).reshape(tok_rows, local_width)
    projected = jnp.dot(attended, out_weight.T, preferred_element_type=jnp.float32)
    own_width = residual.shape[1]
    full_sum = lax.psum(projected, "tensor")
    own_sum = lax.dynamic_slice_in_dim(full_sum, lax.axis_index("tensor") * own_width, own_width, 1)
    layer_out = (own_sum + residual.astype(jnp.float32)).astype(jnp.bfloat16)
    out_float = layer_out.astype(jnp.float32)
    upstream_float = upstream.astype(jnp.float32)
    scaled = upstream_float * norm_gain[None, :]
    square_sum, inner_sum = lax.psum(
        (jnp.sum(out_float * out_float, axis=1), jnp.sum(scaled * out_float, axis=1)), "tensor"
    )
    row_rms = jnp.sqrt(square_sum / D + epsilon)[:, None]
    normed = out_float / row_rms
    row_inner = inner_sum[:, None] / (row_rms * D)
    grad_residual = (
        residual_grad.astype(jnp.float32) + (scaled - normed * row_inner) / row_rms
    ).astype(jnp.bfloat16)
    grad_gain = lax.psum(jnp.sum(upstream_float * normed, axis=0), "dp")
    grad_full = lax.all_gather(grad_residual, "tensor", axis=1, tiled=True)
    grad_attended = jnp.dot(grad_full, out_weight, preferred_element_type=jnp.float32).astype(
        jnp.bfloat16
    )
    contract_rows = (((0,), (0,)), ((), ()))
    received = lax.all_to_all(grad_full, "dp", split_axis=1, concat_axis=0, tiled=True)
    grad_out_weight = lax.dot_general(
        received,
        lax.all_gather(attended, "dp", axis=0, tiled=True),
        contract_rows,
        preferred_element_type=jnp.float32,
    )
    grad_heads = grad_attended.reshape(head_shape)
    grad_value = jnp.einsum(
        "shqk,sqhd->skhd", chances_low, grad_heads, preferred_element_type=jnp.float32
    ).astype(jnp.bfloat16)
    grad_chances = jnp.einsum(
        "sqhd,skhd->shqk", grad_heads, value_heads, preferred_element_type=jnp.float32
    )
    row_delta = jnp.sum(chances * grad_chances, axis=-1, keepdims=True)
    grad_scores = (chances * (grad_chances - row_delta) * score_scale).astype(jnp.bfloat16)
    grad_query = jnp.einsum(
        "shqk,skhd->sqhd", grad_scores, key_heads, preferred_element_type=jnp.float32
    ).astype(jnp.bfloat16)
    grad_key = jnp.einsum(
        "shqk,sqhd->skhd", grad_scores, query_heads, preferred_element_type=jnp.float32
    ).astype(jnp.bfloat16)
    return (
        layer_out,
        grad_residual,
        grad_query.reshape(tok_rows, local_width),
        grad_key.reshape(tok_rows, local_width),
        grad_value.reshape(tok_rows, local_width),
        grad_out_weight,
        grad_gain,
    )


def solution(mesh):
    placed = (
        P("dp", "tensor"),
        P("dp", "tensor"),
        P("dp", "tensor"),
        P("dp", None),
        P("dp", "tensor"),
        P(None, "tensor"),
        P("tensor"),
        P("dp", "tensor"),
        P("dp", "tensor"),
    )
    return jax.shard_map(
        shards,
        mesh=mesh,
        in_specs=placed,
        out_specs=(
            P("dp", "tensor"),
            P("dp", "tensor"),
            P("dp", "tensor"),
            P("dp", "tensor"),
            P("dp", "tensor"),
            P("dp", "tensor"),
            P("tensor"),
        ),
        check_vma=False,
    )
```

profile of v0, /device:TPU:0, one launch (start us, length us, event | category | flops | bytes accessed | tf_op | source)
XLA Modules:
  0.0 635.0 jit_solution(9114788977476758334)
XLA Ops:
  7.2 0.0 copy-start.6
  7.2 0.0 all-reduce.2.cloned.1.call-start
  7.2 2.8 copy.35
  10.1 0.0 copy-done.6
  10.1 0.0 copy-start.1
  10.1 0.1 fusion.40
  10.3 4.4 copy.31
  14.7 3.9 copy.32
  18.6 10.4 %fusion.47 = (f32[20,384]{1,0:T(8,128)S(1)}, f32[20,384,384]{1,2,0:T(8,128)}) fusion(pred[384,384]{0,1:T(8,128)(4,1)S(1)} %fusion.40, bf16[384,20,128]{0,2,1:T(8,128)(2,1)} %bitcast.58, bf16[384,20,128]{0,2,1:T(8,128)(2,1)} %bitcast.60), kind=kOutput, calls=%fused_computation.48 | convolution fusion | flops 766771584 | bytes 15906816 | tf_op jit(solution)/shard_map/sub | solution.py:45
  29.0 0.0 copy-done.1
  29.0 7.1 %fusion.26 = bf16[20,384,128]{1,2,0:T(8,128)(2,1)} fusion(bf16[384,20,128]{0,2,1:T(8,128)(2,1)S(1)} %bitcast.51, f32[20,384,384]{1,2,0:T(8,128)} %get-tuple-element.26, f32[20,384]{1,0:T(8,128)S(1)} %get-tuple-element.25), kind=kOutput, calls=%fused_computation.32 | convolution fusion | flops 761856000 | bytes 15759360 | tf_op jit(solution)/shard_map/shqk,skhd->sqhd/dot_general | solution.py:48
  36.1 17.8 %fusion.48 = f32[384,5120]{1,0:T(8,128)} fusion(bf16[384,2560]{0,1:T(8,128)(2,1)} %bitcast.56, bf16[5120,2560]{1,0:T(8,128)(2,1)} %param.14), kind=kOutput, calls=%fused_computation.49 | convolution fusion | flops 10066329600 | bytes 36044800 | tf_op jit(solution)/shard_map/dot_general | solution.py:52
  53.9 0.0 all-reduce.2.cloned.1.call-update
  54.0 0.2 all-gather.3.cloned.1.call-start
  54.2 0.0 copy-start.5
  54.2 189.9 %all-reduce.2.cloned.1.call-done = f32[384,5120]{1,0:T(8,128)} async-done(((f32[384,5120]{1,0:T(8,128)}), f32[384,5120]{1,0:T(8,128)}) %all-reduce.2.cloned.1.call-update) | async-done | bytes 7864336 | tf_op jit(solution)/shard_map/psum | solution.py:54
  244.1 3.4 fusion.19
  247.5 0.0 copy-start
  247.5 4.9 psum.29
  252.5 0.0 copy-done.5
  252.5 3.1 fusion.18
  255.5 4.9 psum.30
  260.5 5.0 fusion.21
  265.4 0.0 copy-done
  265.4 0.0 all-gather.3.cloned.1.call-update
  265.5 0.0 all-gather.5.cloned.1.call-start
  265.5 0.7 all-gather.5.cloned.1.call-update
  266.2 53.2 %all-gather.3.cloned.1.call-done = bf16[384,5120]{1,0:T(8,128)(2,1)} async-done(((bf16[384,2560]{1,0:T(8,128)(2,1)}), bf16[384,5120]{1,0:T(8,128)(2,1)}) %all-gather.3.cloned.1.call-update) | async-done | bytes 3932176 | tf_op jit(solution)/shard_map/all_gather | solution.py:70
  319.4 6.3 copy.43
  325.7 5.7 all-to-all-start
  331.3 185.8 %psum.31 = f32[2560]{0:T(1024)} all-reduce(f32[2560]{0:T(1024)S(1)} %get-tuple-element.21), channel_id=1, replica_groups=mesh['dp'=16,'tensor'=2] {'dp'}, use_global_device_ids=true, to_apply=%region_9.10 | all-reduce | flops 2560 | bytes 20480 | tf_op jit(solution)/shard_map/psum | solution.py:69
  517.1 17.4 %convolution_convert_fusion = bf16[384,2560]{1,0:T(8,128)(2,1)} fusion(bf16[384,5120]{1,0:T(8,128)(2,1)} %all-gather.3.cloned.1.call-done, bf16[5120,2560]{1,0:T(8,128)(2,1)} %param.14), kind=kOutput, calls=%fused_computation.20 | convolution fusion | flops 10067312640 | bytes 32112640 | tf_op jit(solution)/shard_map/dot_general | solution.py:71
  534.5 0.0 copy-start.2
  534.5 4.2 copy.37
  538.7 0.0 copy-done.2
  538.7 7.6 %fusion.49 = f32[20,384,384]{1,2,0:T(8,128)} fusion(bf16[384,20,128]{0,2,1:T(8,128)(2,1)} %bitcast.53, bf16[384,20,128]{0,2,1:T(8,128)(2,1)S(1)} %bitcast.52), kind=kOutput, calls=%fused_computation.50 | convolution fusion | flops 754974720 | bytes 15728640 | tf_op jit(solution)/shard_map/sqhd,skhd->shqk/dot_general | solution.py:86
  546.3 20.3 %fusion.32 = bf16[20,384,128]{1,2,0:T(8,128)(2,1)} fusion(bf16[384,20,128]{0,2,1:T(8,128)(2,1)} %bitcast.61, f32[20,384,384]{1,2,0:T(8,128)} %fusion.49, f32[20,384,384]{1,2,0:T(8,128)} %get-tuple-element.26, f32[20,384]{1,0:T(8,128)S(1)} %get-tuple-element.25), kind=kOutput, calls=%fused_computation.34 | convolution fusion | flops 776609664 | bytes 27555840 | tf_op jit(solution)/shard_map/shqk,skhd->sqhd/dot_general | solution.py:91
  566.6 0.0 copy-start.4
  566.6 4.1 copy.45
  570.7 0.0 copy-done.4
  570.7 19.7 %fusion.35 = bf16[20,384,128]{1,2,0:T(8,128)(2,1)} fusion(bf16[384,20,128]{0,2,1:T(8,128)(2,1)S(1)} %bitcast.59, f32[20,384,384]{1,2,0:T(8,128)} %fusion.49, f32[20,384,384]{1,2,0:T(8,128)} %get-tuple-element.26, f32[20,384]{1,0:T(8,128)S(1)} %get-tuple-element.25), kind=kOutput, calls=%fused_computation.35 | convolution fusion | flops 776609664 | bytes 27555840 | tf_op jit(solution)/shard_map/shqk,sqhd->skhd/dot_general | solution.py:94
  590.5 4.1 copy.46
  594.6 0.0 copy-done.3
  594.6 7.5 %fusion.29 = bf16[20,128,384]{2,1,0:T(8,128)(2,1)} fusion(bf16[384,20,128]{0,2,1:T(8,128)(2,1)S(1)} %bitcast.54, f32[20,384,384]{1,2,0:T(8,128)} %get-tuple-element.26, f32[20,384]{1,0:T(8,128)S(1)} %get-tuple-element.25), kind=kOutput, calls=%fused_computation.33 | convolution fusion | flops 761856000 | bytes 15759360 | tf_op jit(solution)/shard_map/shqk,sqhd->skhd/dot_general | solution.py:83
  602.1 4.0 copy.47
  606.1 0.0 all-to-all-done
  606.1 4.7 copy.56
  610.8 17.7 %fusion.50 = f32[320,2560]{1,0:T(8,128)} fusion(bf16[6144,320]{0,1:T(8,128)(2,1)} %bitcast.55, bf16[6144,2560]{0,1:T(8,128)(2,1)} %all-gather.5.cloned.1.call-done), kind=kOutput, calls=%fused_computation.51 | convolution fusion | flops 10066329600 | bytes 38666240 | tf_op jit(solution)/shard_map/dot_general | solution.py:76
  (5 shorter events, 0.0 us)
Async XLA Ops:
  7.2 2.9 copy-start.6
  7.2 236.9 %all-reduce.2.cloned.1.call-start = ((), (), s32[]{:S(2)}) async-start(), calls=%async_computation.1 | async-start | bytes 15728640 | tf_op jit(solution)/shard_map/psum | solution.py:54
  10.1 18.9 %copy-start.1 = (bf16[384,2560]{0,1:T(8,128)(2,1)}, bf16[384,2560]{0,1:T(8,128)(2,1)S(1)}, u32[]{:S(2)}) copy-start(bf16[384,2560]{0,1:T(8,128)(2,1)S(1)} %copy.35) | copy-start | bytes 5898244
  54.0 265.4 %all-gather.3.cloned.1.call-start = ((), (), s32[]{:S(2)}) async-start(), calls=%async_computation.2 | async-start | bytes 5898240 | tf_op jit(solution)/shard_map/all_gather | solution.py:70
  54.2 198.3 %copy-start.5 = (f32[2560]{0:T(1024)S(1)}, f32[2560]{0:T(1024)}, u32[]{:S(2)}) copy-start(f32[2560]{0:T(1024)} %param.15) | copy-start | bytes 30724
  247.5 17.9 %copy-start = (bf16[384,2560]{1,0:T(8,128)(2,1)}, bf16[384,2560]{1,0:T(8,128)(2,1)S(1)}, u32[]{:S(2)}) copy-start(bf16[384,2560]{1,0:T(8,128)(2,1)S(1)} %get-tuple-element.24) | copy-start | bytes 5898244
  265.5 345.3 %all-gather.5.cloned.1.call-start = ((), (), s32[]{:S(2)}) async-start(), calls=%async_computation.3 | async-start | bytes 33423360 | tf_op jit(solution)/shard_map/all_gather | solution.py:78
  325.7 280.4 %all-to-all-start = ((bf16[384,16,320]{0,2,1:T(8,128)(2,1)}), bf16[384,16,320]{0,2,1:T(8,128)(2,1)}, u32[]{:S(2)}, u32[]{:S(2)}) async-start(bf16[384,16,320]{0,2,1:T(8,128)(2,1)} %bitcast.50), calls=%async_computation | async-start | bytes 7864320 | tf_op jit(solution)/shard_map/all_to_all | solution.py:75
  534.5 4.2 copy-start.2
  566.6 4.1 copy-start.4
  590.4 4.1 copy-start.3
Sparse Core Ops, SparseCore 0:
  54.1 189.9 all-reduce.1
  265.6 53.7 all-gather.2
  321.5 231.1 all-gather.4
where the time goes:
time: 636 us; the launch traced here: 635 us
  waiting for transfers between devices  244 us (38%)
  blocking collectives  196 us (31%)
  matrix products  126 us (20%)
  local copies, waits for them, and re-layouts  38.5 us (6%)
  between operations  13.8 us (2%)
  other arithmetic  11.7 us (2%)
    psum x1, waiting for transfers between devices, shards(): full_sum = lax.psum(projected, 'tensor')  190 us
    psum x1, blocking collectives, shards(): grad_gain = lax.psum(jnp.sum(upstream_float * normed, axis=0), 'dp')  186 us
    all_gather x1, waiting for transfers between devices, shards(): grad_full = lax.all_gather(grad_residual, 'tensor', axis=1, tiled=True)  53.2 us
    unnamed x20, local copies, waits for them, and re-layouts  23.4 us
    dot_general x1, matrix products, shards(): jnp.einsum('shqk,skhd->sqhd', grad_scores, key_heads, preferred_element_t...  20.3 us
    dot_general x1, matrix products, shards(): jnp.einsum('shqk,sqhd->skhd', grad_scores, query_heads, preferred_element...  19.7 us
    dot_general x1, matrix products, shards(): jnp.dot(attended, out_weight.T, preferred_element_type=jnp.float32)  17.8 us
    dot_general x1, matrix products, shards(): lax.dot_general(received, lax.all_gather(attended, 'dp', axis=0, tiled=Tr...  17.7 us
  transfers between devices with their start and end apart: 4, of which 2 were waited for; matrix products, arithmetic and copies ran while one was open for 16% of the time, Pallas kernels for 0%

commit v1 on v0

--- a/solution.py
+++ b/solution.py
@@ -66,7 +66,7 @@
     grad_residual = (
         residual_grad.astype(jnp.float32) + (scaled - normed * row_inner) / row_rms
     ).astype(jnp.bfloat16)
-    grad_gain = lax.psum(jnp.sum(upstream_float * normed, axis=0), "dp")
+    grad_gain = jnp.sum(lax.all_gather(jnp.sum(upstream_float * normed, axis=0), "dp"), axis=0)
     grad_full = lax.all_gather(grad_residual, "tensor", axis=1, tiled=True)
     grad_attended = jnp.dot(grad_full, out_weight, preferred_element_type=jnp.float32).astype(
         jnp.bfloat16

time: 636 us -> 595 us (0.936)
  blocking collectives: 196 us -> 154 us
    psum x1 -> x0, blocking collectives: 186 us -> none  [shards(): grad_gain = lax.psum(jnp.sum(upstream_float * normed, axis=0), 'dp')]
    all_gather x0 -> x1, blocking collectives: none -> 144 us  [shards(): lax.all_gather(jnp.sum(upstream_float * normed, axis=0), 'dp')]
    unnamed x20 -> x21, local copies, waits for them, and re-layouts: 23.4 us -> 23.5 us
  transfers between devices with their start and end apart: 4 -> 4, of which waited for: 2 -> 2; matrix products, arithmetic and copies ran while one was open for 16% -> 17% of each run, Pallas kernels for 0% -> 0%
where the time goes in v1:
time: 595 us; the launch traced here: 594 us
  waiting for transfers between devices  244 us (41%)
  blocking collectives  154 us (26%)
  matrix products  126 us (21%)
  local copies, waits for them, and re-layouts  38.6 us (6%)
  between operations  13.8 us (2%)
  other arithmetic  12.4 us (2%)
  starting transfers between devices  5.96 us (1%)
    psum x1, waiting for transfers between devices, shards(): full_sum = lax.psum(projected, 'tensor')  190 us
    all_gather x1, blocking collectives, shards(): lax.all_gather(jnp.sum(upstream_float * normed, axis=0), 'dp')  144 us
    all_gather x1, waiting for transfers between devices, shards(): grad_full = lax.all_gather(grad_residual, 'tensor', axis=1, tiled=True)  53.2 us
    unnamed x21, local copies, waits for them, and re-layouts  23.5 us
    dot_general x1, matrix products, shards(): jnp.einsum('shqk,skhd->sqhd', grad_scores, key_heads, preferred_element_t...  20.3 us
    dot_general x1, matrix products, shards(): jnp.einsum('shqk,sqhd->skhd', grad_scores, query_heads, preferred_element...  19.7 us
    dot_general x1, matrix products, shards(): jnp.dot(attended, out_weight.T, preferred_element_type=jnp.float32)  17.8 us
    dot_general x1, matrix products, shards(): lax.dot_general(received, lax.all_gather(attended, 'dp', axis=0, tiled=Tr...  17.7 us
  transfers between devices with their start and end apart: 4, of which 2 were waited for; matrix products, arithmetic and copies ran while one was open for 17% of the time, Pallas kernels for 0%

profile of v1, /device:TPU:0, one launch (start us, length us, event | category | flops | bytes accessed | tf_op | source)
XLA Modules:
  0.0 593.6 jit_solution(14160028943839079372)
XLA Ops:
  7.2 0.0 copy-start.6
  7.2 0.0 all-reduce.2.cloned.1.call-start
  7.2 2.8 copy.52
  10.1 0.0 copy-done.6
  10.1 0.0 copy-start.1
  10.1 0.1 fusion.40
  10.3 4.4 copy.48
  14.7 3.9 copy.49
  18.6 10.4 %fusion.47 = (f32[20,384]{1,0:T(8,128)S(1)}, f32[20,384,384]{1,2,0:T(8,128)}) fusion(pred[384,384]{0,1:T(8,128)(4,1)S(1)} %fusion.40, bf16[384,20,128]{0,2,1:T(8,128)(2,1)} %bitcast.58, bf16[384,20,128]{0,2,1:T(8,128)(2,1)} %bitcast.60), kind=kOutput, calls=%fused_computation.48 | convolution fusion | flops 766771584 | bytes 15906816 | tf_op jit(solution)/shard_map/sub | solution.py:45
  29.0 0.0 copy-done.1
  29.0 7.1 %fusion.26 = bf16[20,384,128]{1,2,0:T(8,128)(2,1)} fusion(bf16[384,20,128]{0,2,1:T(8,128)(2,1)S(1)} %bitcast.51, f32[20,384,384]{1,2,0:T(8,128)} %get-tuple-element.33, f32[20,384]{1,0:T(8,128)S(1)} %get-tuple-element.32), kind=kOutput, calls=%fused_computation.32 | convolution fusion | flops 761856000 | bytes 15759360 | tf_op jit(solution)/shard_map/shqk,skhd->sqhd/dot_general | solution.py:48
  36.1 17.8 %fusion.48 = f32[384,5120]{1,0:T(8,128)} fusion(bf16[384,2560]{0,1:T(8,128)(2,1)} %bitcast.56, bf16[5120,2560]{1,0:T(8,128)(2,1)} %param.14), kind=kOutput, calls=%fused_computation.49 | convolution fusion | flops 10066329600 | bytes 36044800 | tf_op jit(solution)/shard_map/dot_general | solution.py:52
  53.9 0.0 all-reduce.2.cloned.1.call-update
  54.0 0.2 all-gather.5.cloned.1.call-start
  54.2 0.0 copy-start.5
  54.2 189.9 %all-reduce.2.cloned.1.call-done = f32[384,5120]{1,0:T(8,128)} async-done(((f32[384,5120]{1,0:T(8,128)}), f32[384,5120]{1,0:T(8,128)}) %all-reduce.2.cloned.1.call-update) | async-done | bytes 7864336 | tf_op jit(solution)/shard_map/psum | solution.py:54
  244.1 3.4 fusion.19
  247.5 0.0 copy-start
  247.5 4.9 psum.22
  252.5 0.0 copy-done.5
  252.5 3.1 fusion.18
  255.5 4.9 psum.23
  260.5 5.0 fusion.21
  265.4 0.0 copy-done
  265.4 0.0 all-gather.5.cloned.1.call-update
  265.5 0.0 all-gather.7.cloned.1.call-start
  265.5 0.7 all-gather.7.cloned.1.call-update
  266.2 53.2 %all-gather.5.cloned.1.call-done = bf16[384,5120]{1,0:T(8,128)(2,1)} async-done(((bf16[384,2560]{1,0:T(8,128)(2,1)}), bf16[384,5120]{1,0:T(8,128)(2,1)}) %all-gather.5.cloned.1.call-update) | async-done | bytes 3932176 | tf_op jit(solution)/shard_map/all_gather | solution.py:70
  319.4 6.3 %copy.60 = bf16[384,5120]{0,1:T(8,128)(2,1)} copy(bf16[384,5120]{1,0:T(8,128)(2,1)} %all-gather.5.cloned.1.call-done) | data formatting | bytes 7864320 | tf_op jit(solution)/shard_map/all_gather | solution.py:70
  325.7 5.7 all-to-all-start
  331.3 143.7 %all-gather.1 = f32[16,1,2560]{2,1,0:T(1,128)S(1)} all-gather(f32[1,1,2560]{2,1,0:T(1,128)S(1)} %reshape.177), channel_id=2, replica_groups=mesh['dp'=16,'tensor'=2] {'dp'}, dimensions={0}, use_global_device_ids=true | all-gather | bytes 174080 | tf_op jit(solution)/shard_map/all_gather | solution.py:69
  475.0 0.7 reduce_sum.59
  475.7 17.3 %convolution_convert_fusion = bf16[384,2560]{1,0:T(8,128)(2,1)} fusion(bf16[384,5120]{1,0:T(8,128)(2,1)} %all-gather.5.cloned.1.call-done, bf16[5120,2560]{1,0:T(8,128)(2,1)} %param.14), kind=kOutput, calls=%fused_computation.20 | convolution fusion | flops 10067312640 | bytes 32112640 | tf_op jit(solution)/shard_map/dot_general | solution.py:71
  493.1 0.0 copy-start.2
  493.1 4.2 copy.54
  497.3 0.0 copy-done.2
  497.3 7.6 %fusion.49 = f32[20,384,384]{1,2,0:T(8,128)} fusion(bf16[384,20,128]{0,2,1:T(8,128)(2,1)} %bitcast.53, bf16[384,20,128]{0,2,1:T(8,128)(2,1)S(1)} %bitcast.52), kind=kOutput, calls=%fused_computation.50 | convolution fusion | flops 754974720 | bytes 15728640 | tf_op jit(solution)/shard_map/sqhd,skhd->shqk/dot_general | solution.py:86
  504.9 20.3 %fusion.32 = bf16[20,384,128]{1,2,0:T(8,128)(2,1)} fusion(bf16[384,20,128]{0,2,1:T(8,128)(2,1)} %bitcast.61, f32[20,384,384]{1,2,0:T(8,128)} %fusion.49, f32[20,384,384]{1,2,0:T(8,128)} %get-tuple-element.33, f32[20,384]{1,0:T(8,128)S(1)} %get-tuple-element.32), kind=kOutput, calls=%fused_computation.34 | convolution fusion | flops 776609664 | bytes 27555840 | tf_op jit(solution)/shard_map/shqk,skhd->sqhd/dot_general | solution.py:91
  525.2 4.1 copy.62
  529.3 0.0 copy-done.4
  529.3 19.7 %fusion.35 = bf16[20,384,128]{1,2,0:T(8,128)(2,1)} fusion(bf16[384,20,128]{0,2,1:T(8,128)(2,1)S(1)} %bitcast.59, f32[20,384,384]{1,2,0:T(8,128)} %fusion.49, f32[20,384,384]{1,2,0:T(8,128)} %get-tuple-element.33, f32[20,384]{1,0:T(8,128)S(1)} %get-tuple-element.32), kind=kOutput, calls=%fused_computation.35 | convolution fusion | flops 776609664 | bytes 27555840 | tf_op jit(solution)/shard_map/shqk,sqhd->skhd/dot_general | solution.py:94
  549.1 4.1 copy.63
  553.2 0.0 copy-done.3
  553.2 7.5 %fusion.29 = bf16[20,128,384]{2,1,0:T(8,128)(2,1)} fusion(bf16[384,20,128]{0,2,1:T(8,128)(2,1)S(1)} %bitcast.54, f32[20,384,384]{1,2,0:T(8,128)} %get-tuple-element.33, f32[20,384]{1,0:T(8,128)S(1)} %get-tuple-element.32), kind=kOutput, calls=%fused_computation.33 | convolution fusion | flops 761856000 | bytes 15759360 | tf_op jit(solution)/shard_map/shqk,sqhd->skhd/dot_general | solution.py:83
  560.7 4.0 copy.64
  564.7 0.0 all-to-all-done
  564.7 4.7 copy.73
  569.4 17.7 %fusion.50 = f32[320,2560]{1,0:T(8,128)} fusion(bf16[6144,320]{0,1:T(8,128)(2,1)} %bitcast.55, bf16[6144,2560]{0,1:T(8,128)(2,1)} %all-gather.7.cloned.1.call-done), kind=kOutput, calls=%fused_computation.51 | convolution fusion | flops 10066329600 | bytes 38666240 | tf_op jit(solution)/shard_map/dot_general | solution.py:76
  (7 shorter events, 0.1 us)
Async XLA Ops:
  7.2 2.9 copy-start.6
  7.2 236.9 %all-reduce.2.cloned.1.call-start = ((), (), s32[]{:S(2)}) async-start(), calls=%async_computation.1 | async-start | bytes 15728640 | tf_op jit(solution)/shard_map/psum | solution.py:54
  10.1 18.9 %copy-start.1 = (bf16[384,2560]{0,1:T(8,128)(2,1)}, bf16[384,2560]{0,1:T(8,128)(2,1)S(1)}, u32[]{:S(2)}) copy-start(bf16[384,2560]{0,1:T(8,128)(2,1)S(1)} %copy.52) | copy-start | bytes 5898244
  54.0 265.4 %all-gather.5.cloned.1.call-start = ((), (), s32[]{:S(2)}) async-start(), calls=%async_computation.2 | async-start | bytes 5898240 | tf_op jit(solution)/shard_map/all_gather | solution.py:70
  54.2 198.3 %copy-start.5 = (f32[2560]{0:T(1024)S(1)}, f32[2560]{0:T(1024)}, u32[]{:S(2)}) copy-start(f32[2560]{0:T(1024)} %param.15) | copy-start | bytes 30724
  247.5 17.9 %copy-start = (bf16[384,2560]{1,0:T(8,128)(2,1)}, bf16[384,2560]{1,0:T(8,128)(2,1)S(1)}, u32[]{:S(2)}) copy-start(bf16[384,2560]{1,0:T(8,128)(2,1)S(1)} %get-tuple-element.31) | copy-start | bytes 5898244
  265.5 303.9 %all-gather.7.cloned.1.call-start = ((), (), s32[]{:S(2)}) async-start(), calls=%async_computation.3 | async-start | bytes 33423360 | tf_op jit(solution)/shard_map/all_gather | solution.py:78
  325.7 239.1 %all-to-all-start = ((bf16[384,16,320]{0,2,1:T(8,128)(2,1)}), bf16[384,16,320]{0,2,1:T(8,128)(2,1)}, u32[]{:S(2)}, u32[]{:S(2)}) async-start(bf16[384,16,320]{0,2,1:T(8,128)(2,1)} %bitcast.50), calls=%async_computation | async-start | bytes 7864320 | tf_op jit(solution)/shard_map/all_to_all | solution.py:75
  493.1 4.2 copy-start.2
  525.2 4.1 copy-start.4
  549.1 4.1 copy-start.3
Sparse Core Ops, SparseCore 0:
  54.1 189.9 all-reduce.1
  265.6 53.7 all-gather.4
  321.5 231.1 all-gather.6
